TPU v7x, 32 devices: a 4x4x1 block of a 4x4x8 slice. The times are simulated.
32 devices in a mesh: data: 1 (over z), col: 4 (over y), row: 8 (over x, core).
Axes of the slice: x: 4, y: 4, z: 1, core: 2. Of those that a mesh axis runs over, the one named last changes fastest.
The devices are a block of a 4x4x8 slice.
Arguments:
- tokens: bfloat16 [4096, 6144], P(('data', 'row'), 'col')
- w_qkv: bfloat16 [6144, 8192], P('row', 'col')
- w_out: bfloat16 [6144, 6144], P('row', 'col')
- doc_ids: int32 [4096], P(('data', 'row'))
Outputs:
- output: bfloat16 [4096, 6144], P(('data', 'row'), 'col')
All inputs are finite; a program needn't handle non-finite values.
Results may differ from a plain program's by a relative error of at most 0.0039.
Values are sent between devices in bfloat16 or wider.
A program may use at most 768 MiB of HBM per device.

v0:
```python
import jax
import jax.numpy as jnp
from jax import lax
from jax.sharding import PartitionSpec as P

HEAD_DIM = 128


def block_size(row_count, score_width):
    q_blk = row_count
    while q_blk % 16 == 0 and q_blk * score_width > 4194304:
        q_blk = q_blk // 2
    return q_blk


def solution(mesh):
    score_scale = HEAD_DIM ** -0.5

    def local_block(tokens, w_qkv, w_out, doc_ids):
        rows_loc, cols_loc = tokens.shape
        heads_loc = cols_loc // HEAD_DIM
        groups_loc = (w_qkv.shape[1] - cols_loc) // (2 * HEAD_DIM)
        group_ratio = heads_loc // groups_loc
        x_panel = lax.all_gather(tokens, "col", axis=1, tiled=True)
        w_panel = lax.all_gather(w_qkv, "row", axis=0, tiled=True)
        qkv_rows = jnp.dot(x_panel, w_panel, preferred_element_type=jnp.float32).astype(jnp.bfloat16)
        qkv_rows = qkv_rows.reshape(rows_loc, groups_loc, group_ratio + 2, HEAD_DIM)
        kv_all = lax.all_gather(qkv_rows[:, :, group_ratio:, :], "row", axis=0, tiled=True)
        seg_all = lax.all_gather(doc_ids, "row", axis=0, tiled=True)
        seq_len = kv_all.shape[0]
        key_rows = kv_all[:, :, 0, :]
        value_rows = kv_all[:, :, 1, :]
        q_blk = block_size(rows_loc, heads_loc * seq_len)
        n_steps = rows_loc // q_blk
        q_steps = qkv_rows[:, :, :group_ratio, :].reshape(n_steps, q_blk, groups_loc, group_ratio, HEAD_DIM)

        def attend(block_in):
            q_part, seg_part = block_in
            scores = jnp.einsum("qgrd,kgd->qgrk", q_part, key_rows, preferred_element_type=jnp.float32) * score_scale
            same_doc = seg_part[:, None, None, None] == seg_all[None, None, None, :]
            scores = jnp.where(same_doc, scores, -jnp.inf)
            weights = jax.nn.softmax(scores, axis=-1).astype(jnp.bfloat16)
            context = jnp.einsum("qgrk,kgd->qgrd", weights, value_rows, preferred_element_type=jnp.float32)
            return context.astype(jnp.bfloat16)

        context = lax.map(attend, (q_steps, doc_ids.reshape(n_steps, q_blk)))
        context = context.reshape(rows_loc, cols_loc)
        o_panel = lax.all_gather(context, "col", axis=1, tiled=True)
        wo_panel = lax.all_gather(w_out, "row", axis=0, tiled=True)
        return jnp.dot(o_panel, wo_panel, preferred_element_type=jnp.float32).astype(jnp.bfloat16)

    row_spec = P(("data", "row"), "col")
    weight_spec = P("row", "col")
    return jax.shard_map(local_block, mesh=mesh, in_specs=(row_spec, weight_spec, weight_spec, P(("data", "row"))), out_specs=row_spec, check_vma=False)
```

profile of v0, /device:TPU:97, one launch (start us, length us, event | category | flops | bytes accessed | tf_op | source)
XLA Modules:
  0.0 496.3 jit_solution(3720366705216124687)
XLA Ops:
  6.6 0.7 all-gather.7.cloned.1.call-update
  7.4 0.7 all-gather.9.cloned.1.call-update
  8.2 67.6 %all-gather.7.cloned.1.call-done = bf16[512,6144]{1,0:T(8,128)(2,1)} async-done(((bf16[512,1536]{1,0:T(8,128)(2,1)}), bf16[512,6144]{1,0:T(8,128)(2,1)}) %all-gather.7.cloned.1.call-update) | async-done | bytes 6291472 | tf_op jit(solution)/shard_map/all_gather | solution.py:24
  75.8 121.1 %all-gather.9.cloned.1.call-done = bf16[6144,2048]{1,0:T(8,128)(2,1)} async-done(((bf16[768,2048]{1,0:T(8,128)(2,1)}), bf16[6144,2048]{1,0:T(8,128)(2,1)}) %all-gather.9.cloned.1.call-update) | async-done | bytes 25165840 | tf_op jit(solution)/shard_map/all_gather | solution.py:25
  197.0 19.7 %fusion.27 = bf16[64,8,16,128]{3,1,2,0:T(8,128)(2,1)S(1)} fusion(bf16[512,6144]{1,0:T(8,128)(2,1)} %all-gather.7.cloned.1.call-done, bf16[6144,2048]{1,0:T(8,128)(2,1)} %all-gather.9.cloned.1.call-done), kind=kOutput, calls=%fused_computation.29 | convolution fusion | flops 12885950464 | bytes 33554432 | tf_op jit(solution)/shard_map/dot_general | solution.py:26
  216.7 0.6 copy.20
  217.3 0.5 slice.17
  217.8 0.9 copy.18
  218.8 0.6 all-gather.15.cloned.1.call-update
  219.6 17.8 %all-gather = s32[8,1,512]{2,1,0:T(1,128)S(1)} all-gather(s32[1,1,512]{2,1,0:T(1,128)S(1)} %bitcast.73), channel_id=1, replica_groups=mesh['data'=1,'col'=4,'row'=8] {'row'}, dimensions={0}, use_global_device_ids=true | all-gather | bytes 18432 | tf_op jit(solution)/shard_map/all_gather | solution.py:29
  237.4 1.5 copy.17
  238.9 10.2 %all-gather.11.cloned.1.call-done = bf16[4096,2,2,128]{3,0,1,2:T(8,128)(2,1)} async-done(((bf16[512,2,2,128]{3,0,1,2:T(8,128)(2,1)}), bf16[4096,2,2,128]{3,0,1,2:T(8,128)(2,1)}) %all-gather.11.cloned.1.call-update) | async-done | bytes 4194320 | tf_op jit(solution)/shard_map/all_gather | solution.py:28
  249.2 3.8 slice_bitcast_fusion
  252.9 152.6 %while.10 = (s32[]{:T(128)}, bf16[8,64,2,6,128]{4,1,3,2,0:T(8,128)(2,1)}, s32[8,64]{1,0:T(8,128)S(1)}, s32[4096]{0:T(1024)S(1)}, bf16[8,64,2,6,128]{4,1,0,3,2:T(...) while((s32[]{:T(128)}, ...), condition=%wide.region_3.4_spmd, body=%wide.region_0.3_spmd.sunk | while | flops 1636143104 | bytes 55467864 | solution.py:46
  252.9 2.7 fusion.43
  255.7 0.2 broadcast_compare_fusion.2
  255.9 8.4 %fusion.45 = (f32[64,2,6]{0,2,1:T(8,128)S(1)}, f32[64,2,6,4096]{3,0,2,1:T(8,128)}) fusion(f32[2,64,6,4096]{3,1,2,0:T(8,128)S(1)} %fusion.43, pred[64,4096]{1,0:T(8,128)(4,1)S(1)} %broadcast_compare_fusion.2), kind=kOutput, calls=%fused_computation.30.clone.1 | output fusion | flops 18878464 | bytes 25431040 | tf_op jit(solution)/shard_map/while/body/eval_jaxpr/sub | solution.py:42
  264.3 7.7 %fusion.46 = bf16[8,64,2,6,128]{4,1,3,2,0:T(8,128)(2,1)} fusion(bf16[8,64,2,6,128]{4,1,3,2,0:T(8,128)(2,1)} %get-tuple-element.131, s32[]{:T(128)} %get-tuple-element.130, bf16[4096,2,128]{2,0,1:T(8,128)(2,1)} %get-tuple-element.144, f32[64,2,6,4096]{3,0,2,1:T(8,128)} %get-tuple-element.120, f32[64,2,6]{0,2,1:T(8,128)S(1)} %get-tuple-element.121), kind=kOutput, calls=%fused_computation.16.clone.1 | convolution fusion | flops 811696128 | bytes 14880256 | tf_op jit(solution)/shard_map/while/body/eval_jaxpr/qgrk,kgd->qgrd/dot_general | solution.py:43
  272.0 2.7 fusion.43
  274.8 0.2 broadcast_compare_fusion.2
  275.0 8.4 %fusion.45 = (f32[64,2,6]{0,2,1:T(8,128)S(1)}, f32[64,2,6,4096]{3,0,2,1:T(8,128)}) fusion(f32[2,64,6,4096]{3,1,2,0:T(8,128)S(1)} %fusion.43, pred[64,4096]{1,0:T(8,128)(4,1)S(1)} %broadcast_compare_fusion.2), kind=kOutput, calls=%fused_computation.30.clone.1 | output fusion | flops 18878464 | bytes 25431040 | tf_op jit(solution)/shard_map/while/body/eval_jaxpr/sub | solution.py:42
  283.4 7.7 %fusion.46 = bf16[8,64,2,6,128]{4,1,3,2,0:T(8,128)(2,1)} fusion(bf16[8,64,2,6,128]{4,1,3,2,0:T(8,128)(2,1)} %get-tuple-element.131, s32[]{:T(128)} %get-tuple-element.130, bf16[4096,2,128]{2,0,1:T(8,128)(2,1)} %get-tuple-element.144, f32[64,2,6,4096]{3,0,2,1:T(8,128)} %get-tuple-element.120, f32[64,2,6]{0,2,1:T(8,128)S(1)} %get-tuple-element.121), kind=kOutput, calls=%fused_computation.16.clone.1 | convolution fusion | flops 811696128 | bytes 14880256 | tf_op jit(solution)/shard_map/while/body/eval_jaxpr/qgrk,kgd->qgrd/dot_general | solution.py:43
  291.1 2.7 fusion.43
  293.8 0.2 broadcast_compare_fusion.2
  294.1 8.4 %fusion.45 = (f32[64,2,6]{0,2,1:T(8,128)S(1)}, f32[64,2,6,4096]{3,0,2,1:T(8,128)}) fusion(f32[2,64,6,4096]{3,1,2,0:T(8,128)S(1)} %fusion.43, pred[64,4096]{1,0:T(8,128)(4,1)S(1)} %broadcast_compare_fusion.2), kind=kOutput, calls=%fused_computation.30.clone.1 | output fusion | flops 18878464 | bytes 25431040 | tf_op jit(solution)/shard_map/while/body/eval_jaxpr/sub | solution.py:42
  302.5 7.7 %fusion.46 = bf16[8,64,2,6,128]{4,1,3,2,0:T(8,128)(2,1)} fusion(bf16[8,64,2,6,128]{4,1,3,2,0:T(8,128)(2,1)} %get-tuple-element.131, s32[]{:T(128)} %get-tuple-element.130, bf16[4096,2,128]{2,0,1:T(8,128)(2,1)} %get-tuple-element.144, f32[64,2,6,4096]{3,0,2,1:T(8,128)} %get-tuple-element.120, f32[64,2,6]{0,2,1:T(8,128)S(1)} %get-tuple-element.121), kind=kOutput, calls=%fused_computation.16.clone.1 | convolution fusion | flops 811696128 | bytes 14880256 | tf_op jit(solution)/shard_map/while/body/eval_jaxpr/qgrk,kgd->qgrd/dot_general | solution.py:43
  310.2 2.7 fusion.43
  312.9 0.2 broadcast_compare_fusion.2
  313.1 8.4 %fusion.45 = (f32[64,2,6]{0,2,1:T(8,128)S(1)}, f32[64,2,6,4096]{3,0,2,1:T(8,128)}) fusion(f32[2,64,6,4096]{3,1,2,0:T(8,128)S(1)} %fusion.43, pred[64,4096]{1,0:T(8,128)(4,1)S(1)} %broadcast_compare_fusion.2), kind=kOutput, calls=%fused_computation.30.clone.1 | output fusion | flops 18878464 | bytes 25431040 | tf_op jit(solution)/shard_map/while/body/eval_jaxpr/sub | solution.py:42
  321.6 7.7 %fusion.46 = bf16[8,64,2,6,128]{4,1,3,2,0:T(8,128)(2,1)} fusion(bf16[8,64,2,6,128]{4,1,3,2,0:T(8,128)(2,1)} %get-tuple-element.131, s32[]{:T(128)} %get-tuple-element.130, bf16[4096,2,128]{2,0,1:T(8,128)(2,1)} %get-tuple-element.144, f32[64,2,6,4096]{3,0,2,1:T(8,128)} %get-tuple-element.120, f32[64,2,6]{0,2,1:T(8,128)S(1)} %get-tuple-element.121), kind=kOutput, calls=%fused_computation.16.clone.1 | convolution fusion | flops 811696128 | bytes 14880256 | tf_op jit(solution)/shard_map/while/body/eval_jaxpr/qgrk,kgd->qgrd/dot_general | solution.py:43
  329.2 2.7 fusion.43
  332.2 8.4 %fusion.45 = (f32[64,2,6]{0,2,1:T(8,128)S(1)}, f32[64,2,6,4096]{3,0,2,1:T(8,128)}) fusion(f32[2,64,6,4096]{3,1,2,0:T(8,128)S(1)} %fusion.43, pred[64,4096]{1,0:T(8,128)(4,1)S(1)} %broadcast_compare_fusion.2), kind=kOutput, calls=%fused_computation.30.clone.1 | output fusion | flops 18878464 | bytes 25431040 | tf_op jit(solution)/shard_map/while/body/eval_jaxpr/sub | solution.py:42
  340.6 7.7 %fusion.46 = bf16[8,64,2,6,128]{4,1,3,2,0:T(8,128)(2,1)} fusion(bf16[8,64,2,6,128]{4,1,3,2,0:T(8,128)(2,1)} %get-tuple-element.131, s32[]{:T(128)} %get-tuple-element.130, bf16[4096,2,128]{2,0,1:T(8,128)(2,1)} %get-tuple-element.144, f32[64,2,6,4096]{3,0,2,1:T(8,128)} %get-tuple-element.120, f32[64,2,6]{0,2,1:T(8,128)S(1)} %get-tuple-element.121), kind=kOutput, calls=%fused_computation.16.clone.1 | convolution fusion | flops 811696128 | bytes 14880256 | tf_op jit(solution)/shard_map/while/body/eval_jaxpr/qgrk,kgd->qgrd/dot_general | solution.py:43
  348.3 2.7 fusion.43
  351.1 0.2 broadcast_compare_fusion.2
  351.3 8.4 %fusion.45 = (f32[64,2,6]{0,2,1:T(8,128)S(1)}, f32[64,2,6,4096]{3,0,2,1:T(8,128)}) fusion(f32[2,64,6,4096]{3,1,2,0:T(8,128)S(1)} %fusion.43, pred[64,4096]{1,0:T(8,128)(4,1)S(1)} %broadcast_compare_fusion.2), kind=kOutput, calls=%fused_computation.30.clone.1 | output fusion | flops 18878464 | bytes 25431040 | tf_op jit(solution)/shard_map/while/body/eval_jaxpr/sub | solution.py:42
  359.7 7.7 %fusion.46 = bf16[8,64,2,6,128]{4,1,3,2,0:T(8,128)(2,1)} fusion(bf16[8,64,2,6,128]{4,1,3,2,0:T(8,128)(2,1)} %get-tuple-element.131, s32[]{:T(128)} %get-tuple-element.130, bf16[4096,2,128]{2,0,1:T(8,128)(2,1)} %get-tuple-element.144, f32[64,2,6,4096]{3,0,2,1:T(8,128)} %get-tuple-element.120, f32[64,2,6]{0,2,1:T(8,128)S(1)} %get-tuple-element.121), kind=kOutput, calls=%fused_computation.16.clone.1 | convolution fusion | flops 811696128 | bytes 14880256 | tf_op jit(solution)/shard_map/while/body/eval_jaxpr/qgrk,kgd->qgrd/dot_general | solution.py:43
  367.4 2.7 fusion.43
  370.4 8.4 %fusion.45 = (f32[64,2,6]{0,2,1:T(8,128)S(1)}, f32[64,2,6,4096]{3,0,2,1:T(8,128)}) fusion(f32[2,64,6,4096]{3,1,2,0:T(8,128)S(1)} %fusion.43, pred[64,4096]{1,0:T(8,128)(4,1)S(1)} %broadcast_compare_fusion.2), kind=kOutput, calls=%fused_computation.30.clone.1 | output fusion | flops 18878464 | bytes 25431040 | tf_op jit(solution)/shard_map/while/body/eval_jaxpr/sub | solution.py:42
  378.8 7.7 %fusion.46 = bf16[8,64,2,6,128]{4,1,3,2,0:T(8,128)(2,1)} fusion(bf16[8,64,2,6,128]{4,1,3,2,0:T(8,128)(2,1)} %get-tuple-element.131, s32[]{:T(128)} %get-tuple-element.130, bf16[4096,2,128]{2,0,1:T(8,128)(2,1)} %get-tuple-element.144, f32[64,2,6,4096]{3,0,2,1:T(8,128)} %get-tuple-element.120, f32[64,2,6]{0,2,1:T(8,128)S(1)} %get-tuple-element.121), kind=kOutput, calls=%fused_computation.16.clone.1 | convolution fusion | flops 811696128 | bytes 14880256 | tf_op jit(solution)/shard_map/while/body/eval_jaxpr/qgrk,kgd->qgrd/dot_general | solution.py:43
  386.5 2.7 fusion.43
  389.2 0.2 broadcast_compare_fusion.2
  389.4 8.4 %fusion.45 = (f32[64,2,6]{0,2,1:T(8,128)S(1)}, f32[64,2,6,4096]{3,0,2,1:T(8,128)}) fusion(f32[2,64,6,4096]{3,1,2,0:T(8,128)S(1)} %fusion.43, pred[64,4096]{1,0:T(8,128)(4,1)S(1)} %broadcast_compare_fusion.2), kind=kOutput, calls=%fused_computation.30.clone.1 | output fusion | flops 18878464 | bytes 25431040 | tf_op jit(solution)/shard_map/while/body/eval_jaxpr/sub | solution.py:42
  397.9 7.7 %fusion.46 = bf16[8,64,2,6,128]{4,1,3,2,0:T(8,128)(2,1)} fusion(bf16[8,64,2,6,128]{4,1,3,2,0:T(8,128)(2,1)} %get-tuple-element.131, s32[]{:T(128)} %get-tuple-element.130, bf16[4096,2,128]{2,0,1:T(8,128)(2,1)} %get-tuple-element.144, f32[64,2,6,4096]{3,0,2,1:T(8,128)} %get-tuple-element.120, f32[64,2,6]{0,2,1:T(8,128)S(1)} %get-tuple-element.121), kind=kOutput, calls=%fused_computation.16.clone.1 | convolution fusion | flops 811696128 | bytes 14880256 | tf_op jit(solution)/shard_map/while/body/eval_jaxpr/qgrk,kgd->qgrd/dot_general | solution.py:43
  405.6 2.5 copy.13
  408.1 2.6 reshape.49
  410.7 62.6 %all-gather.13.cloned.1.call-done = bf16[512,6144]{1,0:T(8,128)(2,1)} async-done(((bf16[512,1536]{1,0:T(8,128)(2,1)}), bf16[512,6144]{1,0:T(8,128)(2,1)}) %all-gather.13.cloned.1.call-update) | async-done | bytes 6291472 | tf_op jit(solution)/shard_map/all_gather | solution.py:48
  473.3 16.4 %convolution_convert_fusion.1 = bf16[512,1536]{1,0:T(8,128)(2,1)} fusion(bf16[512,6144]{1,0:T(8,128)(2,1)} %all-gather.13.cloned.1.call-done, bf16[6144,1536]{1,0:T(8,128)(2,1)} %all-gather.15.cloned.1.call-done), kind=kOutput, calls=%fused_computation.26 | convolution fusion | flops 9664462848 | bytes 26738688 | tf_op jit(solution)/shard_map/dot_general | solution.py:50
  (22 shorter events, 0.9 us)
Async XLA Ops:
  6.5 69.3 %all-gather.7.cloned.1.call-start = ((), (), s32[]{:S(2)}) async-start(), calls=%async_computation | async-start | bytes 7864320 | tf_op jit(solution)/shard_map/all_gather | solution.py:24
  7.3 189.6 %all-gather.9.cloned.1.call-start = ((), (), s32[]{:S(2)}) async-start(), calls=%async_computation.1 | async-start | bytes 28311552 | tf_op jit(solution)/shard_map/all_gather | solution.py:25
  8.1 241.0 %all-gather.11.cloned.1.call-start = ((), (), s32[]{:S(2)}) async-start(), calls=%async_computation.2 | async-start | bytes 4718592 | tf_op jit(solution)/shard_map/all_gather | solution.py:28
  216.7 2.8 copy-start
  218.8 192.0 %all-gather.15.cloned.1.call-start = ((), (), s32[]{:S(2)}) async-start(), calls=%async_computation.4 | async-start | bytes 21233664 | tf_op jit(solution)/shard_map/all_gather | solution.py:49
  219.4 253.9 %all-gather.13.cloned.1.call-start = ((), (), s32[]{:S(2)}) async-start(), calls=%async_computation.3 | async-start | bytes 7864320 | tf_op jit(solution)/shard_map/all_gather | solution.py:48
Sparse Core Ops, SparseCore 0:
  8.9 66.8 all-gather.6
  77.4 119.5 all-gather.8
  218.9 30.2 all-gather.10
  250.6 91.4 all-gather.14
  410.8 62.4 all-gather.12
where the time goes:
time: 497 us; the launch traced here: 496 us
  waiting for transfers between devices  264 us (53%)
  matrix products  119 us (24%)
  other arithmetic  69.1 us (14%)
  blocking collectives  17.8 us (4%)
  between operations  13.2 us (3%)
  local copies, waits for them, and re-layouts  12.6 us (3%)
    all_gather x1, waiting for transfers between devices, local_block(): w_panel = lax.all_gather(w_qkv, 'row', axis=0, tiled=True)  121 us
    all_gather x1, waiting for transfers between devices, local_block(): x_panel = lax.all_gather(tokens, 'col', axis=1, tiled=True)  67.6 us
    sub x8, other arithmetic, attend(): weights = jax.nn.softmax(scores, axis=-1).astype(jnp.bfloat16)  67.5 us
    all_gather x1, waiting for transfers between devices, local_block(): o_panel = lax.all_gather(context, 'col', axis=1, tiled=True)  62.6 us
    dot_general x8, matrix products, attend(): jnp.einsum('qgrk,kgd->qgrd', weights, value_rows, preferred_element_type=...  61.5 us
    dot_general x8, matrix products, attend(): jnp.einsum('qgrd,kgd->qgrk', q_part, key_rows, preferred_element_type=jnp...  21.8 us
    dot_general x1, matrix products, local_block(): jnp.dot(x_panel, w_panel, preferred_element_type=jnp.float32)  19.7 us
    all_gather x1, blocking collectives, local_block(): seg_all = lax.all_gather(doc_ids, 'row', axis=0, tiled=True)  17.8 us
  transfers between devices with their start and end apart: 5, of which 4 were waited for; matrix products, arithmetic and copies ran while one was open for 33% of the time, Pallas kernels for 0%

commit v1 on v0

v1 whole, which is shorter than its diff:
```python
import functools
import math

import jax
import jax.numpy as jnp
from jax import lax
from jax.experimental import pallas as pl
from jax.experimental.pallas import tpu as pltpu
from jax.sharding import PartitionSpec as P

HEAD_DIM = 128
CHUNK = 256
MESH = pl.DeviceIdType.MESH
LOG2E = math.log2(math.e)
F32, BF16 = jnp.float32, jnp.bfloat16


def block_kernel(
    n_q, n_out,
    tokens, w_qkv, w_out, docs, out,
    wbuf, xbuf, obuf, kvbuf, qbuf, acc, score, stage, docbuf, doc_col,
    wl_sem, ws_sem, wr_sem, xl_sem, xs_sem, xr_sem, kvs_sem, kvr_sem,
    os_sem, or_sem, fl_sem, fs_sem, fr_sem, dl_sem, ds_sem, dr_sem,
):
    rows, k_dev = xbuf.shape[3], xbuf.shape[4]
    n_row = wbuf.shape[1]
    qkv_cols, out_cols = (n_q + 1) * CHUNK, n_out * CHUNK
    n_j = 1 + n_q + n_out

    me, y = lax.axis_index("row"), lax.axis_index("col")
    x, c = lax.div(me, 2), lax.rem(me, 2)
    other = 1 - c
    xr, xl, xo = lax.rem(x + 1, 4), lax.rem(x + 3, 4), lax.rem(x + 2, 4)
    yr, yl, yo = lax.rem(y + 1, 4), lax.rem(y + 3, 4), lax.rem(y + 2, 4)
    partner = {"row": 2 * x + other}
    x_right, x_left = {"row": 2 * xr + c}, {"row": 2 * xl + c}
    y_right, y_left = {"col": yr}, {"col": yl}

    def send(src, dst, s_sem, r_sem, device):
        return pltpu.make_async_remote_copy(
            src_ref=src, dst_ref=dst, send_sem=s_sem, recv_sem=r_sem,
            device_id=device, device_id_type=MESH)

    def same(ref, s_sem, r_sem, device):
        return send(ref, ref, s_sem, r_sem, device)

    def w_source(j, core):
        if j <= n_q:
            col = core * qkv_cols + (n_q * CHUNK if j == 0 else (j - 1) * CHUNK)
            return w_qkv.at[:, pl.ds(pl.multiple_of(col, 128), CHUNK)]
        col = core * out_cols + (j - 1 - n_q) * CHUNK
        return w_out.at[:, pl.ds(pl.multiple_of(col, 128), CHUNK)]

    def w_local(j):
        return pltpu.make_async_copy(w_source(j, c), wbuf.at[j, me], wl_sem.at[j])

    def w_pair(j):
        return send(w_source(j, other), wbuf.at[j, me], ws_sem.at[j, 4], wr_sem.at[j, 4], partner)

    def w_own(j):
        block = wbuf.at[j, pl.ds(2 * x, 2)]
        return (same(block, ws_sem.at[j, 0], wr_sem.at[j, 0], x_right),
                same(block, ws_sem.at[j, 1], wr_sem.at[j, 1], x_left))

    def w_fwd(j):
        return (same(wbuf.at[j, 2 * xl], ws_sem.at[j, 2], wr_sem.at[j, 2], x_right),
                same(wbuf.at[j, 2 * xr + 1], ws_sem.at[j, 3], wr_sem.at[j, 3], x_left))

    def x_local(h):
        return pltpu.make_async_copy(
            tokens.at[:, pl.ds(h * k_dev, k_dev)], xbuf.at[y, c, h], xl_sem.at[h])

    def x_right_own(h):
        return same(xbuf.at[y, c, h], xs_sem.at[h], xr_sem.at[h], y_right)

    def x_left_own(h):
        return same(xbuf.at[y, c, h], xs_sem.at[2 + h], xr_sem.at[2 + h], y_left)

    def x_fwd():
        return (same(xbuf.at[yl, c, 0], xs_sem.at[4], xr_sem.at[4], y_right),
                same(xbuf.at[yr, c, 1], xs_sem.at[5], xr_sem.at[5], y_left))

    def x_pair(k):
        ref = (xbuf.at[y, c], xbuf.at[yl, c], xbuf.at[yr, c], xbuf.at[yo, c, 0], xbuf.at[yo, c, 1])[k]
        return same(ref, xs_sem.at[6 + k], xr_sem.at[6 + k], partner)

    def kv_own():
        return (same(kvbuf.at[x], kvs_sem.at[0], kvr_sem.at[0], x_right),
                same(kvbuf.at[x], kvs_sem.at[1], kvr_sem.at[1], x_left))

    def kv_fwd():
        return (same(kvbuf.at[xl, 0], kvs_sem.at[2], kvr_sem.at[2], x_right),
                same(kvbuf.at[xr, 1], kvs_sem.at[3], kvr_sem.at[3], x_left))

    def o_own(p):
        ref = obuf.at[y, c, p]
        return (same(ref, os_sem.at[p, 0], or_sem.at[p, 0], y_right),
                same(ref, os_sem.at[p, 1], or_sem.at[p, 1], y_left))

    def o_fwd(p):
        return (same(obuf.at[yl, c, p, 0], os_sem.at[p, 2], or_sem.at[p, 2], y_right),
                same(obuf.at[yr, c, p, 1], os_sem.at[p, 3], or_sem.at[p, 3], y_left))

    def o_pair(p, k):
        ref = (obuf.at[y, c, p], obuf.at[yl, c, p], obuf.at[yr, c, p],
               obuf.at[yo, c, p, 0], obuf.at[yo, c, p, 1])[k]
        return same(ref, os_sem.at[p, 4 + k], or_sem.at[p, 4 + k], partner)

    def out_place(jj):
        return out.at[:, pl.ds(pl.multiple_of(c * out_cols + jj * CHUNK, 128), CHUNK)]

    def out_local(jj):
        return pltpu.make_async_copy(stage.at[jj, c], out_place(jj), fl_sem.at[jj])

    def out_pair(jj):
        return send(stage.at[jj, other], out_place(jj), fs_sem.at[jj], fr_sem.at[jj], partner)

    def doc_send(d):
        return same(docbuf.at[me], ds_sem.at[d - 1], dr_sem.at[d - 1], {"row": lax.rem(me + d, n_row)})

    def start(copies):
        for copy in copies:
            copy.start()

    def arrived(copies):
        for copy in copies:
            copy.wait_recv()

    def w_start_own(j):
        w_local(j).wait()
        w_pair(j).wait_recv()
        start(w_own(j))

    def w_relay(j):
        arrived(w_own(j))
        start(w_fwd(j))

    def chip_of(t):
        return lax.rem(x + t + lax.div(t, 2) * (5 - 2 * t), 4)

    def qkv_chunk(j, dst):
        acc[...] = jnp.zeros_like(acc)

        def step(t, carry):
            for half in range(2):
                total = jnp.dot(xbuf[t, half, 0], wbuf[j, 2 * t], preferred_element_type=F32)
                total += jnp.dot(xbuf[t, half, 1], wbuf[j, 2 * t + 1], preferred_element_type=F32)
                acc[half] += total
            return carry

        lax.fori_loop(0, 4, step, 0)
        dst[...] = acc[...].astype(BF16)

    def out_chunk(j, t0, t1):
        if t0 == 0:
            acc[...] = jnp.zeros_like(acc)

        def step(t, carry):
            chip = chip_of(t)
            for half in range(2):
                total = None
                for core in range(2):
                    for p in range(n_q):
                        part = jnp.dot(obuf[chip, core, p, half],
                                       wbuf[j, 2 * chip + core, p * CHUNK:(p + 1) * CHUNK, :],
                                       preferred_element_type=F32)
                        total = part if total is None else total + part
                acc[half] += total
            return carry

        lax.fori_loop(t0, t1, step, 0)

    def out_finish(jj):
        stage[jj] = acc[...].astype(BF16)
        out_pair(jj).start()
        out_local(jj).start()

    q_blk = score.shape[0]
    per_half = rows // q_blk
    tiles = rows // 128 if rows >= 128 else 1
    lanes = rows // tiles
    exp_scale = HEAD_DIM ** -0.5 * LOG2E

    def attend(p):
        def step(u, carry):
            half, r0 = lax.div(u, per_half), pl.multiple_of(lax.rem(u, per_half) * q_blk, q_blk)
            doc_q = doc_col[half, pl.ds(r0, q_blk), :]
            doc_q = jnp.concatenate([doc_q[:, :lanes]] * tiles, axis=1)
            for h in range(2):
                q = qbuf[half, pl.ds(r0, q_blk), h * HEAD_DIM:(h + 1) * HEAD_DIM]
                top = None
                for r in range(n_row):
                    k = kvbuf[r // 2, r % 2, :, :HEAD_DIM]
                    s = lax.dot_general(q, k, (((1,), (1,)), ((), ())), preferred_element_type=F32)
                    s = jnp.where(doc_q == docbuf[r], s, -jnp.inf)
                    score[:, r * rows:(r + 1) * rows] = s
                    for t in range(tiles):
                        part = s[:, t * lanes:(t + 1) * lanes]
                        top = part if top is None else jnp.maximum(top, part)
                top = jnp.max(top, axis=1, keepdims=True)
                total = None
                for r in range(n_row):
                    e = jnp.exp2((score[:, r * rows:(r + 1) * rows] - top) * exp_scale)
                    score[:, r * rows:(r + 1) * rows] = e
                    for t in range(tiles):
                        part = e[:, t * lanes:(t + 1) * lanes]
                        total = part if total is None else total + part
                inv = 1.0 / jnp.sum(total, axis=1, keepdims=True)
                o = None
                for r in range(n_row):
                    weights = (score[:, r * rows:(r + 1) * rows] * inv).astype(BF16)
                    part = jnp.dot(weights, kvbuf[r // 2, r % 2, :, HEAD_DIM:], preferred_element_type=F32)
                    o = part if o is None else o + part
                obuf[y, c, p, half, pl.ds(r0, q_blk), h * HEAD_DIM:(h + 1) * HEAD_DIM] = o.astype(BF16)
            return carry

        lax.fori_loop(0, 2 * per_half, step, 0)

    def o_start(p):
        start(o_own(p))
        o_pair(p, 0).start()

    def o_relay(p):
        right, left = o_own(p)
        f_right, f_left = o_fwd(p)
        right.wait_recv()
        f_right.start()
        o_pair(p, 1).start()
        left.wait_recv()
        f_left.start()
        o_pair(p, 2).start()

    def o_last(p):
        right, left = o_fwd(p)
        right.wait_recv()
        o_pair(p, 3).start()
        left.wait_recv()
        o_pair(p, 4).start()

    doc_load = pltpu.make_async_copy(docs, docbuf.at[me], dl_sem.at[0])
    for h in range(2):
        x_local(h).start()
    for j in range(n_j):
        w_local(j).start()
    doc_load.start()
    barrier = pltpu.get_barrier_semaphore()
    for d in range(1, n_row):
        pl.semaphore_signal(barrier, inc=1, device_id={"row": lax.rem(me + d, n_row)}, device_id_type=MESH)
    for device in (y_right, y_left):
        pl.semaphore_signal(barrier, inc=1, device_id=device, device_id_type=MESH)
    pl.semaphore_wait(barrier, n_row + 1)

    w_pair(0).start()
    x_local(0).wait()
    x_right_own(0).start()
    x_local(1).wait()
    x_left_own(1).start()
    x_right_own(1).start()
    x_left_own(0).start()
    w_pair(1).start()
    w_start_own(0)
    w_start_own(1)
    doc_load.wait()
    for d in range(1, n_row):
        doc_send(d).start()
    for j in range(2, n_j):
        w_pair(j).start()
    x_pair(0).start()

    x_fwd_right, x_fwd_left = x_fwd()
    x_right_own(0).wait_recv()
    x_fwd_right.start()
    x_left_own(1).wait_recv()
    x_fwd_left.start()
    w_relay(0)
    w_start_own(2)
    for d in range(1, n_row):
        doc_send(d).wait_recv()
    for core in range(2):
        row = docbuf[2 * x + core]
        doc_col[core] = jnp.transpose(jnp.broadcast_to(row, (128, rows)), (1, 0))
    x_right_own(1).wait_recv()
    x_pair(1).start()
    x_left_own(0).wait_recv()
    x_pair(2).start()
    w_relay(1)
    x_fwd_right.wait_recv()
    x_pair(3).start()
    x_fwd_left.wait_recv()
    x_pair(4).start()
    for k in range(5):
        x_pair(k).wait_recv()
    arrived(w_fwd(0))
    qkv_chunk(0, kvbuf.at[x])
    start(kv_own())
    w_relay(2)
    arrived(w_fwd(1))
    qkv_chunk(1, qbuf)
    arrived(kv_own())
    start(kv_fwd())
    w_start_own(3)
    w_start_own(4)
    arrived(kv_fwd())
    attend(0)
    o_start(0)
    w_relay(3)
    w_start_own(5)
    arrived(w_fwd(2))
    qkv_chunk(2, qbuf)
    attend(1)
    o_start(1)
    o_relay(0)
    w_relay(4)
    w_start_own(6)
    o_last(0)
    arrived(w_fwd(3))
    qkv_chunk(3, qbuf)
    attend(2)
    o_start(2)
    w_relay(5)
    o_relay(1)
    o_last(1)
    o_relay(2)
    o_last(2)
    w_relay(6)
    for p in range(n_q):
        for k in range(5):
            o_pair(p, k).wait_recv()
    arrived(w_fwd(4))
    out_chunk(4, 0, 4)
    out_finish(0)
    out_chunk(5, 0, 3)
    arrived(w_fwd(5))
    out_chunk(5, 3, 4)
    out_finish(1)
    out_chunk(6, 0, 3)
    arrived(w_fwd(6))
    out_chunk(6, 3, 4)
    out_finish(2)

    for j in range(n_j):
        w_pair(j).wait_send()
        for copy in w_own(j) + w_fwd(j):
            copy.wait_send()
    for h in range(2):
        x_right_own(h).wait_send()
        x_left_own(h).wait_send()
    for copy in x_fwd() + kv_own() + kv_fwd():
        copy.wait_send()
    for k in range(5):
        x_pair(k).wait_send()
    for p in range(n_q):
        for copy in o_own(p) + o_fwd(p):
            copy.wait_send()
        for k in range(5):
            o_pair(p, k).wait_send()
    for d in range(1, n_row):
        doc_send(d).wait_send()
    for jj in range(n_out):
        out_local(jj).wait()
        out_pair(jj).wait_send()
        out_pair(jj).wait_recv()


def solution(mesh):
    n_row, n_col = mesh.shape["row"], mesh.shape["col"]
    assert n_row == 2 * n_col

    def local_block(tokens, w_qkv, w_out, doc_ids):
        rows, _ = tokens.shape
        k_dev = w_qkv.shape[0]
        n_q = w_qkv.shape[1] // (2 * CHUNK) - 1
        n_out = w_out.shape[1] // (2 * CHUNK)
        n_j = 1 + n_q + n_out
        q_blk = min(256, rows)
        dma = pltpu.SemaphoreType.DMA
        any_spec = pl.BlockSpec(memory_space=pl.ANY)
        return pl.pallas_call(
            functools.partial(block_kernel, n_q, n_out),
            out_shape=jax.ShapeDtypeStruct(tokens.shape, BF16),
            in_specs=[any_spec] * 4,
            out_specs=any_spec,
            scratch_shapes=[
                pltpu.VMEM((n_j, n_row, k_dev, CHUNK), BF16),
                pltpu.VMEM((n_col, 2, 2, rows, k_dev), BF16),
                pltpu.VMEM((n_col, 2, n_q, 2, rows, CHUNK), BF16),
                pltpu.VMEM((n_col, 2, rows, CHUNK), BF16),
                pltpu.VMEM((2, rows, CHUNK), BF16),
                pltpu.VMEM((2, rows, CHUNK), F32),
                pltpu.VMEM((q_blk, n_row * rows), F32),
                pltpu.VMEM((n_out, 2, rows, CHUNK), BF16),
                pltpu.VMEM((n_row, 1, rows), jnp.int32),
                pltpu.VMEM((2, rows, 128), jnp.int32),
                dma((n_j,)), dma((n_j, 5)), dma((n_j, 5)),
                dma((2,)), dma((11,)), dma((11,)),
                dma((4,)), dma((4,)),
                dma((n_q, 9)), dma((n_q, 9)),
                dma((n_out,)), dma((n_out,)), dma((n_out,)),
                dma((1,)), dma((n_row - 1,)), dma((n_row - 1,)),
            ],
            compiler_params=pltpu.CompilerParams(
                collective_id=0, has_side_effects=True, vmem_limit_bytes=67043328),
            name="attention_block",
        )(tokens, w_qkv, w_out, doc_ids.reshape(1, rows))

    row_spec = P(("data", "row"), "col")
    weight_spec = P("row", "col")
    return jax.shard_map(local_block, mesh=mesh, in_specs=(row_spec, weight_spec, weight_spec, P(("data", "row"))),
                         out_specs=row_spec, check_vma=False)
```

time: 497 us -> 230 us (0.46)
  waiting for transfers between devices: 264 us -> 0 us
  Pallas kernels: 0 us -> 227 us
  matrix products: 119 us -> 0 us
  other arithmetic: 69.1 us -> 0 us
  blocking collectives: 17.8 us -> 0 us
  between operations: 13.2 us -> 0.01 us
  local copies, waits for them, and re-layouts: 12.6 us -> 2.65 us
    all_gather x5 -> x0, waiting for transfers between devices: 262 us -> none  [the longest x1 121 us: local_block(): w_panel = lax.all_gather(w_qkv, 'row', axis=0, tiled=True)]
    pallas_call x0 -> x1, Pallas kernels: none -> 227 us  [local_block(): pl.pallas_call(functools.partial(block_kernel, n_q, n_out), out_shape=jax...]
    dot_general x18 -> x0, matrix products: 119 us -> none  [the longest x8 61.5 us: attend(): jnp.einsum('qgrk,kgd->qgrd', weights, value_rows, preferred_element_type=...]
    sub x8 -> x0, other arithmetic: 67.5 us -> none  [attend(): weights = jax.nn.softmax(scores, axis=-1).astype(jnp.bfloat16)]
    all_gather x1 -> x0, blocking collectives: 17.8 us -> none  [local_block(): seg_all = lax.all_gather(doc_ids, 'row', axis=0, tiled=True)]
  transfers between devices with their start and end apart: 5 -> 0, of which waited for: 4 -> 0; matrix products, arithmetic and copies ran while one was open for 33% -> 0% of each run, Pallas kernels for 0% -> 0%
where the time goes in v1:
time: 230 us
  Pallas kernels  227 us (99%)
  local copies, waits for them, and re-layouts  2.65 us (1%)
    pallas_call x1, Pallas kernels, local_block(): pl.pallas_call(functools.partial(block_kernel, n_q, n_out), out_shape=jax...  227 us

profile of v1, /device:TPU:97, one launch (start us, length us, event | category | flops | bytes accessed | tf_op | source)
XLA Modules:
  0.0 229.7 jit_solution(11733585566641259634)
XLA Ops:
  0.0 227.1 %attention_block.1 = bf16[512,1536]{1,0:T(8,128)(2,1)} custom-call(bf16[512,1536]{1,0:T(8,128)(2,1)} %tokens.1, bf16[768,2048]{1,0:T(8,128)(2,1)} %w_qkv.1, bf16[768,1536]{1,0:T(8,128)(2,1)} %w_out.1, s32[1,512]{1,0:T(1,128)} %bitcast.1), custom_call_target="tpu_custom_call" | custom-call | tf_op jit(solution)/shard_map/attention_block/pallas_call | solution.py:378
  227.1 2.7 %copy.6 = bf16[512,1536]{1,0:T(8,128)(2,1)} copy(bf16[512,1536]{1,0:T(8,128)(2,1)} %attention_block.1) | data formatting | bytes 3145728

commit v2 on v0

v2 whole, which is shorter than its diff:
```python
import functools
import math
from types import SimpleNamespace

import jax
import jax.numpy as jnp
from jax import lax
from jax.experimental import pallas as pl
from jax.experimental.pallas import tpu as pltpu
from jax.sharding import PartitionSpec as P

HEAD_DIM = 128
CHUNK = 256
MESH = pl.DeviceIdType.MESH
LOG2E = math.log2(math.e)
F32, BF16 = jnp.float32, jnp.bfloat16


def block_kernel(
    n_q, n_out,
    tokens, w_qkv, w_out, docs, out,
    wq, wo, xbuf, obuf, kvbuf, qbuf, acc, score, docbuf, doc_col,
    ql_sem, qs_sem, qr_sem, wl_sem, ws_sem, wr_sem, xl_sem, xs_sem, xr_sem,
    ks_sem, kr_sem, os_sem, or_sem, fl_sem, fs_sem, fr_sem, dl_sem, ds_sem, dr_sem,
):
    rows, k_dev = xbuf.shape[3], xbuf.shape[4]
    n_row = wq.shape[1]
    qkv_cols, out_cols = (n_q + 1) * CHUNK, n_out * CHUNK
    n_j = 1 + n_q
    split = rows // 2

    me, y = lax.axis_index("row"), lax.axis_index("col")
    x, c = lax.div(me, 2), lax.rem(me, 2)
    group = lax.div(x, 2)
    near, mate = x + 1 - 2 * lax.rem(x, 2), 3 - x
    far = 3 - near
    yr, yl, yo = (lax.rem(y + d, 4) for d in (1, 3, 2))
    partner = {"row": 2 * x + 1 - c}
    to_near, to_mate = {"row": 2 * near + c}, {"row": 2 * mate + c}
    right, left = {"col": yr}, {"col": yl}
    others = [lax.rem(me + d, n_row) for d in range(1, n_row)]

    started = []

    def go(*copies):
        for copy in copies:
            copy.start()
            started.append(copy)

    def arrived(*copies):
        for copy in copies:
            copy.wait_recv()

    def make(source, place, s_sem, r_sem, device):
        return pltpu.make_async_remote_copy(
            src_ref=source, dst_ref=place, send_sem=s_sem, recv_sem=r_sem,
            device_id=device, device_id_type=MESH)

    def remote(s_sem, r_sem, **table):
        made = {}
        for i, (name, entry) in enumerate(table.items()):
            made[name] = make(entry[0], entry[-2], s_sem.at[i], r_sem.at[i], entry[-1])
        return SimpleNamespace(**made)

    def q_source(j, g):
        col = g * qkv_cols + (n_q if j == 0 else j - 1) * CHUNK
        return w_qkv.at[:, pl.ds(pl.multiple_of(col, 128), CHUNK)]

    def q_copies(j):
        near_block, mate_block, far_block = (wq.at[j, 2 * chip + c] for chip in (near, mate, far))
        return remote(
            qs_sem.at[j], qr_sem.at[j],
            near=(q_source(j, group), wq.at[j, me], to_near),
            mate=(q_source(j, 1 - group), wq.at[j, me], to_mate),
            relay=(mate_block, to_near),
            pair_own=(q_source(j, group), wq.at[j, me], partner),
            pair_near=(near_block, partner),
            pair_mate=(mate_block, partner),
            pair_far=(far_block, partner))

    def w_source(j, core):
        col = core * out_cols + j * CHUNK
        return w_out.at[:, pl.ds(pl.multiple_of(col, 128), CHUNK)]

    def w_copies(j):
        block_a, block_b = wo.at[j, 2 * x], wo.at[j, 2 * x + 1]
        copies = dict(
            near_a=(block_a, to_near), near_b=(block_b, to_near),
            mate_a=(block_a, to_mate), mate_b=(block_b, to_mate),
            pair=(w_source(j, 1 - c), wo.at[j, me], partner),
            relay_a=(wo.at[j, 2 * mate], to_near))
        if j == n_out - 1:
            copies.update(relay_b=(wo.at[j, 2 * mate + 1], to_near))
        else:
            copies.update(relay_b=(wo.at[j, 2 * near + 1], to_mate))
        return remote(ws_sem.at[j], wr_sem.at[j], **copies)

    def x_half(h):
        return tokens.at[:, pl.ds(h * k_dev, k_dev)]

    x_own = remote(
        xs_sem.at[0], xr_sem.at[0],
        right0=(xbuf.at[0, y, 0], right), left1=(xbuf.at[0, y, 1], left),
        right1=(xbuf.at[0, y, 1], right), left0=(xbuf.at[0, y, 0], left),
        relay_right=(xbuf.at[0, yl, 0], right), relay_left=(xbuf.at[0, yr, 1], left),
        mate0=(x_half(0), xbuf.at[1, y, 0], to_mate), mate1=(x_half(1), xbuf.at[1, y, 1], to_mate))
    x_far = (xbuf.at[s, yo, :, pl.ds(split, split)] for s in range(2))
    x_mate = remote(
        xs_sem.at[1], xr_sem.at[1],
        right0=(xbuf.at[1, y, 0], right), left1=(xbuf.at[1, y, 1], left),
        right1=(xbuf.at[1, y, 1], right), left0=(xbuf.at[1, y, 0], left),
        relay_right=(xbuf.at[1, yl, 0, pl.ds(0, split)], right),
        relay_left=(xbuf.at[1, yr, 1, pl.ds(0, split)], left),
        far=(*x_far, to_mate))

    kv = remote(
        ks_sem, kr_sem,
        own=(kvbuf.at[x, c], to_near), mate=(kvbuf.at[mate, c], to_near),
        pair_own=(kvbuf.at[x, c], partner), pair_mate=(kvbuf.at[mate, c], partner),
        pair_near=(kvbuf.at[near, c], partner), pair_far=(kvbuf.at[far, c], partner))

    def o_copies(p):
        def place(col):
            return obuf.at[col, p, c, 1 - group], obuf.at[col, p, c, group]

        first, second = place(y)
        first_l, second_l = place(yl)
        first_r, second_r = place(yr)
        first_o, second_o = place(yo)
        return remote(
            os_sem.at[p], or_sem.at[p],
            back=(qbuf.at[p, 1], second, to_mate),
            first_right=(first, right), first_left=(first, left),
            second_right=(second, right), second_left=(second, left),
            relay_right=(first_l, right), relay_left=(second_r, left),
            pair_first=(first, partner), pair_second=(second, partner),
            pair_first_l=(first_l, partner), pair_second_l=(second_l, partner),
            pair_first_r=(first_r, partner), pair_second_r=(second_r, partner),
            pair_first_o=(first_o, partner), pair_second_o=(second_o, partner))

    def out_place(j):
        return out.at[:, pl.ds(pl.multiple_of(c * out_cols + j * CHUNK, 128), CHUNK)]

    out_local = [pltpu.make_async_copy(qbuf.at[j, c], out_place(j), fl_sem.at[j]) for j in range(n_out)]
    out_pair = [make(qbuf.at[j, 1 - c], out_place(j), fs_sem.at[j], fr_sem.at[j], partner) for j in range(n_out)]
    doc = [make(docbuf.at[me], docbuf.at[me], ds_sem.at[i], dr_sem.at[i], {"row": other})
           for i, other in enumerate(others)]

    q = [q_copies(j) for j in range(n_j)]
    w = [w_copies(j) for j in range(n_out)]
    o = [o_copies(p) for p in range(n_q)]

    def order(i, t):
        return lax.rem(i + t + lax.div(t, 2) * (5 - 2 * t), 4)

    def clear(i):
        acc[i] = jnp.zeros(acc.shape[1:], F32)

    def qkv_part(s, j, t0, t1):
        if t0 == 0:
            clear(j)

        def step(t, carry):
            col = order(y, t)
            total = jnp.dot(xbuf[s, col, 0], wq[j, 2 * col], preferred_element_type=F32)
            total += jnp.dot(xbuf[s, col, 1], wq[j, 2 * col + 1], preferred_element_type=F32)
            acc[j] += total
            return carry

        lax.fori_loop(t0, t1, step, 0)

    def qkv_store(s, j):
        value = acc[j].astype(BF16)
        if j == 0:
            kvbuf[mate if s else x, c] = value
        else:
            qbuf[j - 1, s] = value

    def out_part(j, start_at, t0, t1, p0, p1):
        if t0 == 0 and p0 == 0:
            clear(2 * j)
            clear(2 * j + 1)

        def step(t, carry):
            col = order(start_at, t)
            for half in range(2):
                total = None
                for g in range(2):
                    for p in range(p0, p1):
                        part = jnp.dot(obuf[col, p, half, g],
                                       wo[j, 2 * col + g, p * CHUNK:(p + 1) * CHUNK, :],
                                       preferred_element_type=F32)
                        total = part if total is None else total + part
                acc[2 * j + half] += total
            return carry

        lax.fori_loop(t0, t1, step, 0)

    def out_finish(j):
        qbuf[j] = acc[2 * j:2 * j + 2].astype(BF16)
        go(out_pair[j])
        out_local[j].start()

    q_blk = score.shape[1]
    per_s = rows // q_blk
    tiles = rows // 128 if rows >= 128 else 1
    lanes = rows // tiles
    exp_scale = HEAD_DIM ** -0.5 * LOG2E

    def query(s, p, u):
        h, r0 = lax.div(u, per_s), pl.multiple_of(lax.rem(u, per_s) * q_blk, q_blk)
        head = pl.ds(pl.multiple_of(h * HEAD_DIM, HEAD_DIM), HEAD_DIM)
        doc_q = doc_col[s, pl.ds(r0, q_blk), :]
        return qbuf[p, s, pl.ds(r0, q_blk), head], jnp.concatenate([doc_q[:, :lanes]] * tiles, axis=1)

    def fold(op, value, total):
        for t in range(tiles):
            part = value[:, t * lanes:(t + 1) * lanes]
            total = part if total is None else op(total, part)
        return total

    def scores(slot, r, q, doc_q, top):
        k = kvbuf[r // 2, r % 2, :, :HEAD_DIM]
        sc = lax.dot_general(q, k, (((1,), (1,)), ((), ())), preferred_element_type=F32)
        sc = jnp.where(doc_q == docbuf[r], sc, -jnp.inf)
        score[slot, :, r * rows:(r + 1) * rows] = sc
        return fold(jnp.maximum, sc, top)

    def first_scores(s, p):
        q, doc_q = query(s, p, 0)
        top = None
        for r in range(n_row):
            top = scores(0, r, q, doc_q, top)
        return jnp.max(top, axis=1, keepdims=True)

    def unit(slot, top, s, p, u, s_b, p_b, u_b):
        q, doc_q = query(s_b, p_b, u_b)
        top_b, total = None, None
        for r in range(n_row):
            part = slice(r * rows, (r + 1) * rows)
            e = jnp.exp2((score[slot, :, part] - top) * exp_scale)
            score[slot, :, part] = e
            total = fold(jnp.add, e, total)
            top_b = scores(1 - slot, r, q, doc_q, top_b)
        inv = 1.0 / jnp.sum(total, axis=1, keepdims=True)
        o = None
        for r in range(n_row):
            weights = (score[slot, :, r * rows:(r + 1) * rows] * inv).astype(BF16)
            part = jnp.dot(weights, kvbuf[r // 2, r % 2, :, HEAD_DIM:], preferred_element_type=F32)
            o = part if o is None else o + part
        o = o.astype(BF16)
        h, r0 = lax.div(u, per_s), pl.multiple_of(lax.rem(u, per_s) * q_blk, q_blk)
        head = pl.ds(pl.multiple_of(h * HEAD_DIM, HEAD_DIM), HEAD_DIM)

        @pl.when(s == 1)
        def _():
            qbuf[p, 1, pl.ds(r0, q_blk), head] = o

        @pl.when(s == 0)
        def _():
            obuf[y, p, c, group, pl.ds(r0, q_blk), head] = o

        return jnp.max(top_b, axis=1, keepdims=True)

    doc_load = pltpu.make_async_copy(docs, docbuf.at[me], dl_sem.at[0])
    x_load = [pltpu.make_async_copy(x_half(h), xbuf.at[0, y, h], xl_sem.at[h]) for h in range(2)]
    q_load = [pltpu.make_async_copy(q_source(j, group), wq.at[j, me], ql_sem.at[j]) for j in range(n_j)]
    w_load = [pltpu.make_async_copy(w_source(j, c), wo.at[j, me], wl_sem.at[j]) for j in range(n_out)]
    for load in [doc_load] + x_load + q_load + w_load:
        load.start()
    barrier = pltpu.get_barrier_semaphore()
    for device in [{"row": other} for other in others] + [right, left]:
        pl.semaphore_signal(barrier, inc=1, device_id=device, device_id_type=MESH)
    pl.semaphore_wait(barrier, n_row + 1)

    doc_load.wait()
    go(*doc)
    go(x_own.mate0, x_own.mate1, q[0].near)
    x_load[0].wait()
    go(x_own.right0)
    x_load[1].wait()
    go(x_own.left1, x_own.right1, x_own.left0)
    go(*(copies.mate for copies in q))
    go(*(copies.near for copies in q[1:]))
    go(*(copies.pair_own for copies in q))
    go(*(copies.pair for copies in w))

    def w_ready(j):
        w_load[j].wait()
        arrived(w[j].pair)

    w_ready(0)
    go(w[0].near_a, w[0].near_b)
    for load in q_load:
        load.wait()
    arrived(*doc)
    for s in range(2):
        row = docbuf[2 * (mate if s else x) + c]
        doc_col[s] = jnp.transpose(jnp.broadcast_to(row, (128, rows)), (1, 0))

    def pass_on(*pairs):
        for there, onward in pairs:
            arrived(there)
            go(onward)

    pass_on((x_own.right0, x_own.relay_right), (x_own.left1, x_own.relay_left),
            (x_own.mate0, x_mate.right0))
    pass_on(*((copies.near, copies.pair_near) for copies in q[:2]))
    arrived(x_own.mate1)
    go(x_mate.left1, x_mate.right1, x_mate.left0)
    pass_on(*((copies.near, copies.pair_near) for copies in q[2:]))
    arrived(x_own.right1, x_own.left0)

    def q_relay(j):
        pass_on((q[j].mate, q[j].relay))
        go(q[j].pair_mate)

    def q_done(j):
        pass_on((q[j].relay, q[j].pair_far))
        arrived(q[j].pair_own, q[j].pair_near, q[j].pair_mate, q[j].pair_far)

    q_relay(0)
    arrived(x_own.relay_right, x_own.relay_left)
    go(x_mate.far)
    q_relay(1)
    q_done(0)
    qkv_part(0, 0, 0, 4)
    qkv_store(0, 0)
    q_relay(2)
    go(w[0].mate_a, w[0].mate_b)
    q_relay(3)
    go(kv.own, kv.pair_own)
    pass_on((x_mate.right0, x_mate.relay_right), (x_mate.left1, x_mate.relay_left))
    w_ready(1)
    go(w[1].mate_a)
    for j in range(1, n_j):
        q_done(j)
        qkv_part(0, j, 0, 4)
        qkv_store(0, j)
    arrived(x_mate.right1, x_mate.left0)
    pass_on((kv.own, kv.pair_near))
    for j in range(n_j):
        qkv_part(1, j, 0, 3)
    w_ready(2)
    arrived(x_mate.far, x_mate.relay_right, x_mate.relay_left)
    for j in range(n_j):
        qkv_part(1, j, 3, 4)
        if j == 1:
            go(kv.mate, kv.pair_mate)
        qkv_store(1, j)
    go(w[1].near_a, w[1].near_b, w[2].near_a, w[2].near_b)
    pass_on((w[0].mate_a, w[0].relay_a), (kv.mate, kv.pair_far))
    arrived(kv.pair_own, kv.pair_mate, kv.pair_near, kv.pair_far)

    def o_first(p):
        arrived(o[p].back)
        go(o[p].first_right, o[p].first_left, o[p].pair_first)

    def o_second(p):
        go(o[p].second_right, o[p].second_left, o[p].pair_second)

    def o_relay(p, is_first):
        if is_first:
            pass_on((o[p].first_right, o[p].relay_right))
        else:
            pass_on((o[p].second_left, o[p].relay_left))

    def o_share(p, is_first):
        if is_first:
            go(o[p].pair_first_l)
            pass_on((o[p].first_left, o[p].pair_first_r))
        else:
            go(o[p].pair_second_r)
            pass_on((o[p].second_right, o[p].pair_second_l))

    def o_last(p):
        pass_on((o[p].relay_right, o[p].pair_first_o), (o[p].relay_left, o[p].pair_second_o))

    def o_done(p, last):
        if last:
            arrived(o[p].pair_first_o, o[p].pair_second_o)
        else:
            arrived(o[p].pair_first, o[p].pair_second, o[p].pair_first_l, o[p].pair_second_l,
                    o[p].pair_first_r, o[p].pair_second_r)

    def after_0():
        go(o[0].back, w[1].mate_b)
        pass_on((w[1].mate_a, w[1].relay_a))

    def after_1():
        o_second(0)
        o_first(0)

    def after_2():
        go(o[1].back, w[2].mate_a)
        o_relay(0, False)

    def after_3():
        o_relay(0, True)
        o_second(1)
        o_first(1)
        o_share(0, False)
        o_share(0, True)
        arrived(w[0].near_b)
        go(w[0].relay_b)

    def after_4():
        arrived(w[1].near_b)
        go(o[2].back, w[2].mate_b, w[1].relay_b)

    def attend(i, top):
        step, u = lax.div(i, 2), per_s * lax.rem(i, 2)
        s, p = 1 - lax.rem(step, 2), lax.div(step, 2)
        later = jnp.minimum(i + 1, 4 * n_q - 1)
        step_b, u_b = lax.div(later, 2), per_s * lax.rem(later, 2)
        top = unit(0, top, s, p, u, s, p, u + 1)
        top = unit(1, top, s, p, u + 1, 1 - lax.rem(step_b, 2), lax.div(step_b, 2), u_b)
        for k, hook in enumerate((after_0, after_1, after_2, after_3, after_4)):
            pl.when(i == 2 * k + 1)(hook)
        pl.when(i == 4 * n_q - 2)(lambda: o_relay(1, False))
        return top

    lax.fori_loop(0, 4 * n_q, attend, first_scores(1, 0))
    o_second(2)
    pass_on((w[2].mate_a, w[2].relay_a))
    o_last(0)
    o_share(1, False)
    o_relay(1, True)
    o_share(1, True)
    o_done(0, False)
    o_done(0, True)
    arrived(w[0].mate_b, w[0].near_a, w[0].relay_a, w[0].relay_b)
    out_part(0, y, 0, 4, 0, 1)
    o_first(2)
    o_relay(2, False)
    arrived(w[1].mate_b, w[1].near_a, w[2].near_a, w[2].near_b)
    o_last(1)
    pass_on((w[2].mate_b, w[2].relay_b))
    o_done(1, False)
    o_done(1, True)
    out_part(0, y, 0, 4, 1, 2)
    out_part(1, x, 0, 3, 0, 2)
    o_relay(2, True)
    o_share(2, False)
    o_share(2, True)
    out_part(2, x, 0, 3, 0, 2)
    o_done(2, False)
    out_part(0, y, 0, 3, 2, 3)
    arrived(w[1].relay_a, w[1].relay_b)
    out_part(1, x, 3, 4, 0, 2)
    out_part(1, y, 0, 3, 2, 3)
    o_last(2)
    arrived(w[2].relay_a, w[2].relay_b)
    out_part(2, x, 3, 4, 0, 2)
    out_part(2, y, 0, 3, 2, 3)
    o_done(2, True)
    for copies in o:
        copies.back.wait_send()
    for j in range(n_out):
        out_part(j, y, 3, 4, 2, 3)
        out_finish(j)

    for copy in started:
        if not any(copy is copies.back for copies in o):
            copy.wait_send()
    for copy in out_local:
        copy.wait()
    arrived(*out_pair)


def solution(mesh):
    n_row, n_col = mesh.shape["row"], mesh.shape["col"]
    assert n_row == 2 * n_col

    def local_block(tokens, w_qkv, w_out, doc_ids):
        rows, _ = tokens.shape
        k_dev = w_qkv.shape[0]
        n_q = w_qkv.shape[1] // (2 * CHUNK) - 1
        n_out = w_out.shape[1] // (2 * CHUNK)
        n_j = 1 + n_q
        q_blk = min(256, rows)
        dma = pltpu.SemaphoreType.DMA
        any_spec = pl.BlockSpec(memory_space=pl.ANY)
        return pl.pallas_call(
            functools.partial(block_kernel, n_q, n_out),
            out_shape=jax.ShapeDtypeStruct(tokens.shape, BF16),
            in_specs=[any_spec] * 4,
            out_specs=any_spec,
            scratch_shapes=[
                pltpu.VMEM((n_j, n_row, k_dev, CHUNK), BF16),
                pltpu.VMEM((n_out, n_row, k_dev, CHUNK), BF16),
                pltpu.VMEM((2, n_col, 2, rows, k_dev), BF16),
                pltpu.VMEM((n_col, n_q, 2, 2, rows, CHUNK), BF16),
                pltpu.VMEM((n_col, 2, rows, CHUNK), BF16),
                pltpu.VMEM((n_q, 2, rows, CHUNK), BF16),
                pltpu.VMEM((max(n_j, 2 * n_out), rows, CHUNK), F32),
                pltpu.VMEM((2, q_blk, n_row * rows), F32),
                pltpu.VMEM((n_row, 1, rows), jnp.int32),
                pltpu.VMEM((2, rows, 128), jnp.int32),
                dma((n_j,)), dma((n_j, 7)), dma((n_j, 7)),
                dma((n_out,)), dma((n_out, 7)), dma((n_out, 7)),
                dma((2,)), dma((2, 8)), dma((2, 8)),
                dma((6,)), dma((6,)),
                dma((n_q, 15)), dma((n_q, 15)),
                dma((n_out,)), dma((n_out,)), dma((n_out,)),
                dma((1,)), dma((n_row - 1,)), dma((n_row - 1,)),
            ],
            compiler_params=pltpu.CompilerParams(
                collective_id=0, has_side_effects=True, vmem_limit_bytes=67043328),
            name="attention_block",
        )(tokens, w_qkv, w_out, doc_ids.reshape(1, rows))

    row_spec = P(("data", "row"), "col")
    weight_spec = P("row", "col")
    return jax.shard_map(local_block, mesh=mesh, in_specs=(row_spec, weight_spec, weight_spec, P(("data", "row"))),
                         out_specs=row_spec, check_vma=False)
```

time: 497 us -> 203 us (0.41)
  waiting for transfers between devices: 264 us -> 0 us
  Pallas kernels: 0 us -> 201 us
  matrix products: 119 us -> 0 us
  other arithmetic: 69.1 us -> 0 us
  blocking collectives: 17.8 us -> 0 us
  between operations: 13.2 us -> 0.01 us
  local copies, waits for them, and re-layouts: 12.6 us -> 2.65 us
    all_gather x5 -> x0, waiting for transfers between devices: 262 us -> none  [the longest x1 121 us: local_block(): w_panel = lax.all_gather(w_qkv, 'row', axis=0, tiled=True)]
    pallas_call x0 -> x1, Pallas kernels: none -> 201 us  [local_block(): pl.pallas_call(functools.partial(block_kernel, n_q, n_out), out_shape=jax...]
    dot_general x18 -> x0, matrix products: 119 us -> none  [the longest x8 61.5 us: attend(): jnp.einsum('qgrk,kgd->qgrd', weights, value_rows, preferred_element_type=...]
    sub x8 -> x0, other arithmetic: 67.5 us -> none  [attend(): weights = jax.nn.softmax(scores, axis=-1).astype(jnp.bfloat16)]
    all_gather x1 -> x0, blocking collectives: 17.8 us -> none  [local_block(): seg_all = lax.all_gather(doc_ids, 'row', axis=0, tiled=True)]
  transfers between devices with their start and end apart: 5 -> 0, of which waited for: 4 -> 0; matrix products, arithmetic and copies ran while one was open for 33% -> 0% of each run, Pallas kernels for 0% -> 0%
where the time goes in v2:
time: 203 us
  Pallas kernels  201 us (99%)
  local copies, waits for them, and re-layouts  2.65 us (1%)
    pallas_call x1, Pallas kernels, local_block(): pl.pallas_call(functools.partial(block_kernel, n_q, n_out), out_shape=jax...  201 us

profile of v2, /device:TPU:97, one launch (start us, length us, event | category | flops | bytes accessed | tf_op | source)
XLA Modules:
  0.0 203.2 jit_solution(5281524363554834659)
XLA Ops:
  0.0 200.6 %attention_block.1 = bf16[512,1536]{1,0:T(8,128)(2,1)} custom-call(bf16[512,1536]{1,0:T(8,128)(2,1)} %tokens.1, bf16[768,2048]{1,0:T(8,128)(2,1)} %w_qkv.1, bf16[768,1536]{1,0:T(8,128)(2,1)} %w_out.1, s32[1,512]{1,0:T(1,128)} %bitcast.1), custom_call_target="tpu_custom_call" | custom-call | tf_op jit(solution)/shard_map/attention_block/pallas_call | solution.py:484
  200.6 2.7 %copy.6 = bf16[512,1536]{1,0:T(8,128)(2,1)} copy(bf16[512,1536]{1,0:T(8,128)(2,1)} %attention_block.1) | data formatting | bytes 3145728
